TPU v7x, 8 devices: a whole 2x2x1 slice. The times are simulated.
8 devices in a mesh: rep: 1 (over z), pp: 8 (over x, y, core).
Axes of the slice: x: 2, y: 2, z: 1, core: 2. Of those that a mesh axis runs over, the one named last changes fastest.
Arguments:
- x: bfloat16 [16, 512, 512], P('rep')
- dy: bfloat16 [16, 512, 512], P('rep')
- w_gate: bfloat16 [8, 512, 1664], P('pp')
- w_up: bfloat16 [8, 512, 1664], P('pp')
- w_down: bfloat16 [8, 1664, 512], P('pp')
Outputs:
- output 1: bfloat16 [8, 512, 1664], P(('rep', 'pp'))
- output 2: bfloat16 [8, 512, 1664], P(('rep', 'pp'))
- output 3: bfloat16 [8, 1664, 512], P(('rep', 'pp'))
All inputs are finite; a program needn't handle non-finite values.
Results may differ from a plain program's by a relative error of at most 0.0274.
Values are sent between devices in bfloat16 or wider.
A program may use at most 2 GiB of HBM per device.

v0:
```python
import jax
import jax.numpy as jnp
from jax import lax
from jax.sharding import PartitionSpec as P

NAMES = ("w_gate", "w_up", "w_down")


def matmul(a, w):
    return jnp.dot(a, w, preferred_element_type=jnp.float32).astype(jnp.bfloat16)


def normed(h):
    wide = h.astype(jnp.float32)
    scale = lax.rsqrt(jnp.mean(wide**2, -1, keepdims=True) + 1e-6)
    return (wide * scale).astype(jnp.bfloat16)


def layer(h, w):
    a = normed(h)
    gate = jnp.dot(a, w["w_gate"], preferred_element_type=jnp.float32)
    up = jnp.dot(a, w["w_up"], preferred_element_type=jnp.float32)
    return h + matmul((jax.nn.silu(gate) * up).astype(jnp.bfloat16), w["w_down"])


def stage(weights, h):
    for number in range(weights["w_gate"].shape[0]):
        h = layer(h, {name: w[number] for name, w in weights.items()})
    return h


def solution(mesh):
    stages = mesh.shape["pp"]
    onward = [(i, i + 1) for i in range(stages - 1)]
    back_again = [(i + 1, i) for i in range(stages - 1)]

    def step(x, dy, *arrays):
        weights = dict(zip(NAMES, arrays, strict=True))
        micro, me = x.shape[0], lax.axis_index("pp")
        kept, came = jnp.zeros_like(x), jnp.zeros_like(x[0])
        for t in range(micro + stages - 1):
            number = jnp.clip(t - me, 0, micro - 1)
            at_work = (t >= me) & (t - me < micro)
            h = jnp.where(me == 0, x[min(t, micro - 1)], came)
            was = lax.dynamic_index_in_dim(kept, number, 0, keepdims=False)
            kept = lax.dynamic_update_index_in_dim(kept, jnp.where(at_work, h, was), number, 0)
            came = lax.ppermute(stage(weights, h), "pp", onward)
        total = {name: jnp.zeros(w.shape, jnp.float32) for name, w in weights.items()}
        came, behind = jnp.zeros_like(x[0]), stages - 1 - me
        for t in range(micro + stages - 1):
            number = jnp.clip(t - behind, 0, micro - 1)
            at_work = (t >= behind) & (t - behind < micro)
            by_y = jnp.where(behind == 0, dy[min(t, micro - 1)], came)
            _, back = jax.vjp(stage, weights, lax.dynamic_index_in_dim(kept, number, 0, keepdims=False))
            by_w, by_h = back(by_y)
            total = {name: total[name] + jnp.where(at_work, by_w[name].astype(jnp.float32), 0.0) for name in NAMES}
            came = lax.ppermute(by_h, "pp", back_again)
        return tuple(total[name].astype(jnp.bfloat16) for name in NAMES)

    return jax.shard_map(
        step,
        mesh=mesh,
        in_specs=(P("rep", None, None),) * 2 + (P("pp", None, None),) * 3,
        out_specs=(P(("rep", "pp"), None, None),) * 3,
        check_vma=False,
    )
```

profile of v0, /device:TPU:2, one launch (start us, length us, event | category | flops | bytes accessed | tf_op | source)
XLA Modules:
  0.0 1146.8 jit_solution(15464966851287130542)
XLA Ops:
  13.9 9.5 collective-permute-done
  28.4 6.2 fusion.809
  36.5 9.5 collective-permute-done.1
  51.0 6.2 fusion.806
  59.1 9.5 collective-permute-done.2
  73.6 6.2 fusion.803
  81.8 9.3 collective-permute-done.3
  96.2 6.2 fusion.800
  104.3 9.5 collective-permute-done.4
  118.7 6.2 fusion.797
  126.9 9.5 collective-permute-done.5
  141.3 6.2 fusion.794
  149.4 9.5 collective-permute-done.6
  163.9 6.2 fusion.791
  172.2 9.3 collective-permute-done.7
  186.5 6.2 fusion.788
  194.6 9.5 collective-permute-done.8
  209.1 6.2 fusion.785
  217.3 9.4 collective-permute-done.9
  231.9 5.7 fusion.782
  321.0 5.7 fusion.770
  343.2 5.8 fusion.767
  365.3 5.7 fusion.764
  387.4 5.7 fusion.761
  409.6 5.7 fusion.758
  431.7 5.7 fusion.755
  453.8 5.8 fusion.752
  475.9 5.7 fusion.749
  508.5 6.2 fusion.1029
  1088.1 19.8 %fusion.393 = bf16[1,512,1664]{2,1,0:T(8,128)(2,1)} fusion(bf16[512,1664]{1,0:T(8,128)(2,1)} %fusion.74, pred[]{:T(512)S(6)} %and.184, bf16[512,1664]{1,0:T(8,128)(2,1)} %convolution_convert_fusion.23, pred[]{:T(512)S(6)} %and.183, bf16[512,1664]{1,0:T(8,128)(2,1)} %convolution_convert_fusion.24, pred[]{:T(512)S(6)} %and.182, ...), kind=kOutput, calls=%fused_computation.620 | convolution fusion | flops 937951232 | bytes 44828700 | tf_op jit(solution)/shard_map/transpose(jvp())/dot_general | solution.py:22
  1107.9 18.3 %fusion.392 = bf16[1,512,1664]{2,1,0:T(8,128)(2,1)} fusion(bf16[512,1664]{1,0:T(8,128)(2,1)} %fusion.75, pred[]{:T(512)S(6)} %and.184, bf16[512,1664]{1,0:T(8,128)(2,1)} %convolution_convert_fusion.46, pred[]{:T(512)S(6)} %and.183, bf16[512,1664]{1,0:T(8,128)(2,1)} %convolution_convert_fusion.48, pred[]{:T(512)S(6)} %and.182, ...), kind=kOutput, calls=%fused_computation.619 | convolution fusion | flops 931987456 | bytes 41420828 | tf_op jit(solution)/shard_map/transpose(jvp())/dot_general | solution.py:21
  1126.2 20.4 %fusion.394 = bf16[1,1664,512]{2,1,0:T(8,128)(2,1)} fusion(pred[]{:T(512)S(6)} %and.184, bf16[1664,512]{1,0:T(8,128)(2,1)} %convolution_convert_fusion.1, pred[]{:T(512)S(6)} %and.183, bf16[1664,512]{1,0:T(8,128)(2,1)} %convolution_convert_fusion.2, pred[]{:T(512)S(6)} %and.182, bf16[1664,512]{1,0:T(8,128)(2,1)} %convolution_convert_fusion.3, ...), kind=kOutput, calls=%fused_computation.621 | convolution fusion | flops 937426944 | bytes 47054872 | tf_op jit(solution)/shard_map/transpose(jvp())/dot_general | solution.py:10
  (694 shorter events, 876.6 us)
Async XLA Ops:
  12.0 11.4 collective-permute-start
  34.6 11.4 collective-permute-start.1
  57.2 11.4 collective-permute-start.2
  79.8 11.4 collective-permute-start.3
  102.4 11.4 collective-permute-start.4
  125.0 11.4 collective-permute-start.5
  147.5 11.4 collective-permute-start.6
  170.1 11.4 collective-permute-start.7
  192.7 11.4 collective-permute-start.8
  215.3 11.4 collective-permute-start.9
  237.6 11.9 %collective-permute-start.10 = (bf16[512,512]{1,0:T(8,128)(2,1)}, bf16[512,512]{1,0:T(8,128)(2,1)S(1)}, u32[]{:S(2)}, u32[]{:S(2)}) collective-permute-start(bf16[512,512]{1,0:T(8,128)(2,1)} %fusion.782), channel_id=1, source_target_pairs={{0,1},{1,2},{2,3},{3,4},{4,5},{5,6},{6,7}} | collective-permute-start | bytes 1572872 | tf_op jit(solution)/shard_map/ppermute | solution.py:47
  260.3 11.4 collective-permute-start.11
  282.5 11.4 collective-permute-start.12
  304.6 11.4 collective-permute-start.13
  326.8 11.4 collective-permute-start.14
  348.9 11.4 collective-permute-start.15
  371.0 11.4 collective-permute-start.16
  393.2 11.4 collective-permute-start.17
  415.3 11.4 collective-permute-start.18
  437.4 11.4 collective-permute-start.19
  459.6 11.4 collective-permute-start.20
  481.7 11.4 collective-permute-start.21
  516.7 65.6 %collective-permute-start.22 = (bf16[512,512]{1,0:T(8,128)(2,1)S(1)}, bf16[512,512]{1,0:T(8,128)(2,1)S(1)}, u32[]{:S(2)}, u32[]{:S(2)}) collective-permute-start(bf16[512,512]{1,0:T(8,128)(2,1)S(1)} %fusion.1146), channel_id=1, source_target_pairs={{1,0},{2,1},{3,2},{4,3},{5,4},{6,5},{7,6}} | collective-permute-start | bytes 1572872 | tf_op jit(solution)/shard_map/ppermute | solution.py:57
  602.3 11.2 collective-permute-start.23
  646.2 11.6 %collective-permute-start.25 = (bf16[512,512]{1,0:T(8,128)(2,1)S(1)}, bf16[512,512]{1,0:T(8,128)(2,1)S(1)}, u32[]{:S(2)}, u32[]{:S(2)}) collective-permute-start(bf16[512,512]{1,0:T(8,128)(2,1)S(1)} %fusion.1143), channel_id=1, source_target_pairs={{1,0},{2,1},{3,2},{4,3},{5,4},{6,5},{7,6}} | collective-permute-start | bytes 1572872 | tf_op jit(solution)/shard_map/ppermute | solution.py:57
  669.4 11.4 collective-permute-start.26
  692.4 11.5 %collective-permute-start.27 = (bf16[512,512]{1,0:T(8,128)(2,1)S(1)}, bf16[512,512]{1,0:T(8,128)(2,1)S(1)}, u32[]{:S(2)}, u32[]{:S(2)}) collective-permute-start(bf16[512,512]{1,0:T(8,128)(2,1)S(1)} %fusion.1141), channel_id=1, source_target_pairs={{1,0},{2,1},{3,2},{4,3},{5,4},{6,5},{7,6}} | collective-permute-start | bytes 1572872 | tf_op jit(solution)/shard_map/ppermute | solution.py:57
  785.5 10.9 collective-permute-start.31
  877.9 10.9 collective-permute-start.35
  970.4 11.0 collective-permute-start.39
  1016.5 10.9 collective-permute-start.41
  1066.8 12.0 %collective-permute-start.43 = (bf16[512,512]{1,0:T(8,128)(2,1)S(1)}, bf16[512,512]{1,0:T(8,128)(2,1)S(1)}, u32[]{:S(2)}, u32[]{:S(2)}) collective-permute-start(bf16[512,512]{1,0:T(8,128)(2,1)S(1)} %fusion.1125), channel_id=1, source_target_pairs={{1,0},{2,1},{3,2},{4,3},{5,4},{6,5},{7,6}} | collective-permute-start | bytes 1572872 | tf_op jit(solution)/shard_map/ppermute | solution.py:57
  (128 other events, 1002.6 us)
where the time goes:
time: 1160 us; the launch traced here: 1150 us
  matrix products  728 us (63%)
  waiting for transfers between devices  126 us (11%)
  starting transfers between devices  119 us (10%)
  other arithmetic  107 us (9%)
  local copies, waits for them, and re-layouts  64.2 us (6%)
    dot_general x90, matrix products, layer(): gate = jnp.dot(a, w['w_gate'], preferred_element_type=jnp.float32)  255 us
    dot_general x68, matrix products, layer(): up = jnp.dot(a, w['w_up'], preferred_element_type=jnp.float32)  239 us
    dot_general x68, matrix products, matmul(): jnp.dot(a, w, preferred_element_type=jnp.float32).astype(jnp.bfloat16)  234 us
    ppermute x22, waiting for transfers between devices, step(): came = lax.ppermute(stage(weights, h), 'pp', onward)  125 us
    ppermute x22, starting transfers between devices, step(): came = lax.ppermute(by_h, 'pp', back_again)  74.5 us
    dynamic_update_slice x23, other arithmetic, step(): lax.dynamic_update_index_in_dim(kept, jnp.where(at_work, h, was), number, 0)  44.1 us
    ppermute x22, starting transfers between devices, step(): came = lax.ppermute(stage(weights, h), 'pp', onward)  44 us
    dynamic_slice x22, local copies, waits for them, and re-layouts, step(): was = lax.dynamic_index_in_dim(kept, number, 0, keepdims=False)  31.6 us
  transfers between devices with their start and end apart: 44, of which 21 were waited for; matrix products, arithmetic and copies ran while one was open for 26% of the time, Pallas kernels for 0%

commit v1 on v0

v1 whole, which is shorter than its diff:
```python
import jax
import jax.numpy as jnp
from jax import lax
from jax.experimental import pallas as pl
from jax.experimental.pallas import tpu as pltpu
from jax.sharding import PartitionSpec as P

F32, BF16 = jnp.float32, jnp.bfloat16
MICRO, T, D, FF, STAGES = 16, 512, 512, 1664, 8
PARTS = 2
C = T // PARTS
CHUNKS = MICRO * PARTS
BLOCKS = FF // 128
RING = 4
SLOTS = 4
AHEAD = (24, 19, 16, 13, 9, 6, 2, 0)
LATE = (0, 1, 2, 0, 3, 3, 3, 3)


def dot(a, b):
    return jnp.dot(a, b, preferred_element_type=F32)


def dot_rows(a, b):
    return lax.dot_general(a, b, (((0,), (0,)), ((), ())), preferred_element_type=F32)


def sigmoid(x):
    return 0.5 * jnp.tanh(0.5 * x) + 0.5


def scale_of(wide):
    return lax.rsqrt(jnp.mean(wide * wide, -1, keepdims=True) + 1e-6)


def forward(h, wgu, wd, act):
    wide = h.astype(F32)
    a = (wide * scale_of(wide)).astype(BF16)
    for j in range(BLOCKS):
        both = dot(a, wgu[:, 256 * j : 256 * j + 256])
        gate, up = both[:, :128], both[:, 128:]
        act[:, 128 * j : 128 * j + 128] = (gate * sigmoid(gate) * up).astype(BF16)
    return h + dot(act[...], wd[...]).astype(BF16)


def backward(h, dy, wgu, wdt, wgut, act, dgu, further):
    wide = h.astype(F32)
    scale = scale_of(wide)
    a = (wide * scale).astype(BF16)
    for start in range(0, BLOCKS, 2):
        blocks = range(start, min(start + 2, BLOCKS))
        by_act = dot(dy, wdt[:, 128 * start : 128 * blocks[-1] + 128]).astype(BF16).astype(F32)
        for j in blocks:
            both = dot(a, wgu[:, 256 * j : 256 * j + 256])
            gate, up = both[:, :128], both[:, 128:]
            by = by_act[:, 128 * (j - start) : 128 * (j - start) + 128]
            s = sigmoid(gate)
            silu = gate * s
            act[:, 128 * j : 128 * j + 128] = (silu * up).astype(BF16)
            dgu[:, 256 * j : 256 * j + 128] = (by * up * (s + silu * (1.0 - s))).astype(BF16)
            dgu[:, 256 * j + 128 : 256 * j + 256] = (by * silu).astype(BF16)
    if not further:
        return None
    by_a = dot(dgu[...], wgut[...]).astype(BF16).astype(F32)
    by_scale = jnp.sum(by_a * wide, -1, keepdims=True)
    by_wide = by_a * scale - wide * (by_scale * scale * scale * scale * (1.0 / D))
    return dy + by_wide.astype(BF16)


def by_weights(h, dy, act, dgu, sum_gu, sum_d):
    wide = h.astype(F32)
    at = (wide * scale_of(wide)).astype(BF16).T
    for j in range(BLOCKS):
        at_j = slice(256 * j, 256 * j + 256)
        sum_gu[:, at_j] += dot(at, dgu[:, at_j]).astype(BF16).astype(F32)
    for start in range(0, FF, 256):
        rows = slice(start, min(start + 256, FF))
        sum_d[rows, :] += dot_rows(act[:, rows], dy).astype(BF16).astype(F32)


def pick(me, values):
    return sum(jnp.where(me == i, v, 0) for i, v in enumerate(values))


def kernel(x, dy, wg_in, wu_in, wd_in, dwg, dwu, dwd, hs, dys, wgu, wd, wdt, wgut, sum_gu, sum_d, act_f, act, dgu, out_f, out_b,
           got_f, got_b, sent_f, sent_b, loaded, stored):
    me = lax.axis_index("pp")
    after, before = lax.rem(me + 1, STAGES), lax.rem(me + STAGES - 1, STAGES)
    first, last = me == 0, me == STAGES - 1
    ahead, late = pick(me, AHEAD), pick(me, LATE)

    def rows(c):
        return pl.ds(pl.multiple_of(c * C, C), C)

    loads = []
    for j in range(BLOCKS):
        loads.append(pltpu.make_async_copy(wg_in.at[0, :, pl.ds(128 * j, 128)], wgu.at[:, pl.ds(256 * j, 128)], loaded.at[2 * j]))
        loads.append(pltpu.make_async_copy(wu_in.at[0, :, pl.ds(128 * j, 128)], wgu.at[:, pl.ds(256 * j + 128, 128)], loaded.at[2 * j + 1]))
    loads.append(pltpu.make_async_copy(wd_in.at[0], wd, loaded.at[2 * BLOCKS]))
    for load in loads:
        load.start()

    def local_f(c):
        return pltpu.make_async_copy(x.at[c // PARTS, pl.ds(pl.multiple_of(lax.rem(c, PARTS) * C, C), C), :], hs.at[rows(c), :], got_f.at[c])

    def local_b(c):
        return pltpu.make_async_copy(dy.at[c // PARTS, pl.ds(pl.multiple_of(lax.rem(c, PARTS) * C, C), C), :], dys.at[rows(c), :], got_b.at[c])

    @pl.when(first)
    def _():
        lax.fori_loop(0, CHUNKS, lambda c, n: (local_f(c).start(), n)[1], 0)

    @pl.when(last)
    def _():
        lax.fori_loop(0, CHUNKS, lambda c, n: (local_b(c).start(), n)[1], 0)

    def send_f(c):
        slot = lax.rem(c, RING)
        return pltpu.make_async_remote_copy(out_f.at[slot], hs.at[rows(c), :], sent_f.at[slot], got_f.at[c],
                                            device_id={"pp": after}, device_id_type=pl.DeviceIdType.MESH)

    def send_b(c):
        slot = lax.rem(c, RING)
        return pltpu.make_async_remote_copy(out_b.at[slot], dys.at[rows(c), :], sent_b.at[slot], got_b.at[c],
                                            device_id={"pp": before}, device_id_type=pl.DeviceIdType.MESH)

    barrier = pltpu.get_barrier_semaphore()

    @pl.when(jnp.logical_not(last))
    def _():
        pl.semaphore_signal(barrier, inc=1, device_id={"pp": after}, device_id_type=pl.DeviceIdType.MESH)

    @pl.when(jnp.logical_not(first))
    def _():
        pl.semaphore_signal(barrier, inc=1, device_id={"pp": before}, device_id_type=pl.DeviceIdType.MESH)

    pl.semaphore_wait(barrier, jnp.where(first | last, 1, 2))
    for load in loads:
        load.wait()

    def step(t, carry):
        @pl.when(t == jnp.where(first, 8, 0))
        def _():
            for j in range(BLOCKS):
                wgut[256 * j : 256 * j + 256, :] = wgu[:, 256 * j : 256 * j + 256].T
            for start in range(0, FF, 256):
                at_s = slice(start, min(start + 256, FF))
                wdt[:, at_s] = wd[at_s, :].T
            sum_gu[...] = jnp.zeros_like(sum_gu)
            sum_d[...] = jnp.zeros_like(sum_d)

        @pl.when((t < CHUNKS) & jnp.logical_not(last))
        def _():
            local_f(t).wait()

            @pl.when(t >= RING)
            def _():
                send_f(t - RING).wait_send()

            out_f[lax.rem(t, RING)] = forward(hs[rows(t), :], wgu, wd, act_f)
            send_f(t).start()

        c = t - ahead

        @pl.when((c >= 0) & (c < CHUNKS))
        def _():
            slot, part = lax.rem(c // PARTS, SLOTS), rows(lax.rem(c, PARTS))
            local_b(c).wait()
            act_c, dgu_c = act.at[slot, part, :], dgu.at[slot, part, :]

            @pl.when(first)
            def _():
                backward(hs[rows(c), :], dys[rows(c), :], wgu, wdt, wgut, act_c, dgu_c, False)

            @pl.when(last)
            def _():
                local_f(c).wait()

            @pl.when(jnp.logical_not(first))
            def _():
                @pl.when(c >= RING)
                def _():
                    send_b(c - RING).wait_send()

                out_b[lax.rem(c, RING)] = backward(hs[rows(c), :], dys[rows(c), :], wgu, wdt, wgut, act_c, dgu_c, True)
                send_b(c).start()

        m = c // PARTS - late

        @pl.when((c >= 0) & (lax.rem(c, PARTS) == PARTS - 1) & (m >= 0) & (m < MICRO))
        def _():
            slot, part = lax.rem(m, SLOTS), pl.ds(pl.multiple_of(m * T, T), T)
            by_weights(hs[part, :], dys[part, :], act.at[slot], dgu.at[slot], sum_gu, sum_d)

        return carry

    lax.fori_loop(0, CHUNKS + ahead + late * PARTS, step, 0)

    @pl.when(jnp.logical_not(last))
    def _():
        lax.fori_loop(CHUNKS - RING, CHUNKS, lambda c, n: (send_f(c).wait_send(), n)[1], 0)

    @pl.when(jnp.logical_not(first))
    def _():
        lax.fori_loop(CHUNKS - RING, CHUNKS, lambda c, n: (send_b(c).wait_send(), n)[1], 0)

    stores = []
    for j in range(BLOCKS):
        cols = slice(256 * j, 256 * j + 256)
        dgu[0, :, cols] = sum_gu[:, cols].astype(BF16)
        stores.append(pltpu.make_async_copy(dgu.at[0, :, pl.ds(256 * j, 128)], dwg.at[0, :, pl.ds(128 * j, 128)], stored.at[2 * j]))
        stores.append(pltpu.make_async_copy(dgu.at[0, :, pl.ds(256 * j + 128, 128)], dwu.at[0, :, pl.ds(128 * j, 128)], stored.at[2 * j + 1]))
        stores[-2].start()
        stores[-1].start()
    wd[...] = sum_d[...].astype(BF16)
    stores.append(pltpu.make_async_copy(wd, dwd.at[0], stored.at[2 * BLOCKS]))
    stores[-1].start()
    for store in stores:
        store.wait()


def solution(mesh):
    def step(x, dy, w_gate, w_up, w_down):
        v, sem = pltpu.VMEM, pltpu.SemaphoreType.DMA
        return pl.pallas_call(
            kernel,
            out_shape=[jax.ShapeDtypeStruct(w.shape, w.dtype) for w in (w_gate, w_up, w_down)],
            in_specs=[pl.BlockSpec(memory_space=pl.ANY)] * 5,
            out_specs=[pl.BlockSpec(memory_space=pl.ANY)] * 3,
            scratch_shapes=[
                v((MICRO * T, D), BF16), v((MICRO * T, D), BF16),
                v((D, 2 * FF), BF16), v((FF, D), BF16), v((D, FF), BF16), v((2 * FF, D), BF16),
                v((D, 2 * FF), F32), v((FF, D), F32),
                v((C, FF), BF16), v((SLOTS, T, FF), BF16), v((SLOTS, T, 2 * FF), BF16),
                v((RING, C, D), BF16), v((RING, C, D), BF16),
                sem((CHUNKS,)), sem((CHUNKS,)), sem((RING,)), sem((RING,)), sem((2 * BLOCKS + 1,)), sem((2 * BLOCKS + 1,)),
            ],
            compiler_params=pltpu.CompilerParams(collective_id=0, has_side_effects=True, vmem_limit_bytes=67043328),
        )(x, dy, w_gate, w_up, w_down)

    return jax.shard_map(
        step,
        mesh=mesh,
        in_specs=(P("rep", None, None),) * 2 + (P("pp", None, None),) * 3,
        out_specs=(P(("rep", "pp"), None, None),) * 3,
        check_vma=False,
    )
```

time: 1160 us -> 265 us (0.23)
  the two profiles are of different devices: /device:TPU:2 before, /device:TPU:0 now
where the time goes in v1:
time: 265 us
  Pallas kernels  258 us (97%)
  local copies, waits for them, and re-layouts  6.15 us (2%)
    pallas_call x1, Pallas kernels, step(): pl.pallas_call(kernel, out_shape=[jax.ShapeDtypeStruct(w.shape, w.dtype)...  258 us
    unnamed x7, local copies, waits for them, and re-layouts  6.15 us

profile of v1, /device:TPU:0, one launch (start us, length us, event | category | flops | bytes accessed | tf_op | source)
XLA Modules:
  0.0 264.7 jit_solution(11521781733573933690)
XLA Ops:
  0.6 257.9 %shard_map.76 = (bf16[1,512,1664]{2,1,0:T(8,128)(2,1)}, bf16[1,512,1664]{2,1,0:T(8,128)(2,1)}, bf16[1,1664,512]{2,1,0:T(8,128)(2,1)}) custom-call(bf16[16,512,512]{2,1,0:T(8,128)(2,1)} %x.1, bf16[16,512,512]{2,1,0:T(8,128)(2,1)} %dy.1, bf16[1,512,1664]{2,1,0:T(8,128)(2,1)} %wg_in.1, bf16[1,512,1664]{2,1,0:T(8,128)(2,1)} %wu_in.1, bf16[1,1664,512]{2,1,0:T(8,128)(2,1)} %wd_in.1), custom_call_target="tpu_custom_call" | custom-call | tf_op jit(solution)/shard_map/pallas_call | solution.py:225
  258.6 0.0 copy-start.1
  258.6 2.9 %copy.11 = bf16[1,512,1664]{2,1,0:T(8,128)(2,1)} copy(bf16[1,512,1664]{2,1,0:T(8,128)(2,1)} %get-tuple-element.6) | data formatting | bytes 3407872
  261.5 0.0 copy-done.1
  261.5 0.0 copy-start
  261.5 1.2 copy.12
  262.7 0.9 copy-done
  263.6 1.2 copy.13
Async XLA Ops:
  258.6 2.9 %copy-start.1 = (bf16[1,512,1664]{2,1,0:T(8,128)(2,1)S(1)}, bf16[1,512,1664]{2,1,0:T(8,128)(2,1)}, u32[]{:S(2)}) copy-start(bf16[1,512,1664]{2,1,0:T(8,128)(2,1)} %get-tuple-element.7) | copy-start | bytes 5111812
  261.5 2.1 copy-start

commit v2 on v1

v2 whole, which is shorter than its diff:
```python
import jax
import jax.numpy as jnp
from jax import lax
from jax.experimental import pallas as pl
from jax.experimental.pallas import tpu as pltpu
from jax.sharding import PartitionSpec as P

F32, BF16 = jnp.float32, jnp.bfloat16
MESH = pl.DeviceIdType.MESH
MICRO, T, D, FF, STAGES = 16, 512, 512, 1664, 8
LAST = STAGES - 1
BLOCKS = FF // 128
LARGE, SMALL = 256, 128
HEAD, TAIL = 1, 1
RING = 4
SLOTS = 3
DEPTH = 6
OVER_F, OVER_B = range(1, 15), range(0)
ORDER = (
    (0x181911911111111111111, 0x12512A831191111A93A19, 0x1622624622C25A235A22C, 0x1626222626622624),
    (0x113311111111111111111, 0x152251113263137112311, 0x162626262626626224522, 0x14622222),
    (0x113311313111111111111, 0x125225326353252531253, 0x122222622262625226353, 0x1446),
    (0x131513313311111111111, 0x152523235227347331253, 0x144622222626263266312),
    (0x131271315331131311111, 0x125232522526316331635, 0x144622226272312737),
    (0x131522713111533331111, 0x172735232631573266313, 0x144622273272312),
    (0x133723512317137223111, 0x172352337527336371316, 0x144622317132),
    (0x166222622622466222222, 0x16224622622266224662),
)
WORD = 7
INIT_AT = 8

PIECES = MICRO * T // 128
TAIL_AT = PIECES - 4 * TAIL
CHUNKS = 4 * HEAD + 2 * (MICRO - HEAD - TAIL) + 4 * TAIL


def steps(numbers):
    digits = []
    for number in numbers:
        while number > 1:
            digits.append(number % 16)
            number //= 16
    return digits


def words(numbers, count):
    digits = steps(numbers)
    digits += [0] * (WORD * count - len(digits))
    return [sum(d * 16**i for i, d in enumerate(digits[at : at + WORD])) for at in range(0, WORD * count, WORD)]


def piece(k):
    middle, tail = 4 * HEAD, CHUNKS - 4 * TAIL
    return jnp.where(k < middle, k, jnp.where(k < tail, middle + 2 * (k - middle), TAIL_AT + k - tail))


def is_small(p):
    return (p < 4 * HEAD) | (p >= TAIL_AT)


def dot(a, b):
    return jnp.dot(a, b, preferred_element_type=F32)


def dot_rows(a, b):
    return lax.dot_general(a, b, (((0,), (0,)), ((), ())), preferred_element_type=F32)


def sigmoid(x):
    return 0.5 * jnp.tanh(0.5 * x) + 0.5


def scale_of(wide):
    return lax.rsqrt(jnp.mean(wide * wide, -1, keepdims=True) + 1e-6)


def hidden(a, j, wgu):
    both = dot(a, wgu[:, 256 * j : 256 * j + 256])
    gate, up = both[:, :128], both[:, 128:]
    s = sigmoid(gate)
    silu = gate * s
    return silu, up * (s + silu * (1.0 - s)), (silu * up).astype(BF16)


def forward(h, wgu, wd, act, kept):
    wide = h.astype(F32)
    a = (wide * scale_of(wide)).astype(BF16)
    for j in range(BLOCKS):
        silu, slope, act[:, 128 * j : 128 * j + 128] = hidden(a, j, wgu)
        kept[:, 256 * j : 256 * j + 128] = slope
        kept[:, 256 * j + 128 : 256 * j + 256] = silu
    return h + dot(act[...], wd[...]).astype(BF16)


def backward(h, dy, wgu, wdt, wgut, act, dgu, kept, further):
    wide = h.astype(F32)
    scale = scale_of(wide)
    if kept is None:
        a = (wide * scale).astype(BF16)
    for start in range(0, BLOCKS, 2):
        blocks = range(start, min(start + 2, BLOCKS))
        by_act = dot(dy, wdt[:, 128 * start : 128 * blocks[-1] + 128]).astype(BF16).astype(F32)
        for j in blocks:
            by = by_act[:, 128 * (j - start) : 128 * (j - start) + 128]
            if kept is None:
                silu, slope, act[:, 128 * j : 128 * j + 128] = hidden(a, j, wgu)
            else:
                slope, silu = kept[:, 256 * j : 256 * j + 128], kept[:, 256 * j + 128 : 256 * j + 256]
            dgu[:, 256 * j : 256 * j + 128] = (by * slope).astype(BF16)
            dgu[:, 256 * j + 128 : 256 * j + 256] = (by * silu).astype(BF16)
    if not further:
        return None
    by_a = dot(dgu[...], wgut[...]).astype(BF16).astype(F32)
    by_scale = jnp.sum(by_a * wide, -1, keepdims=True)
    by_wide = by_a * scale - wide * (by_scale * scale * scale * scale * (1.0 / D))
    return dy + by_wide.astype(BF16)


def by_weights(h, dy, act, dgu, sum_gu, sum_d):
    wide = h.astype(F32)
    at = (wide * scale_of(wide)).astype(BF16).T
    for j in range(BLOCKS):
        at_j = slice(256 * j, 256 * j + 256)
        sum_gu[:, at_j] += dot(at, dgu[:, at_j]).astype(BF16).astype(F32)
    for start in range(0, FF, 256):
        rows = slice(start, min(start + 256, FF))
        sum_d[rows, :] += dot_rows(act[:, rows], dy).astype(BF16).astype(F32)


def pick(me, values):
    return sum(jnp.where(me == i, v, 0) for i, v in enumerate(values))


def kernel(x, dy, wg_in, wu_in, wd_in, dwg, dwu, dwd, kept_far, act_far, hs, dys, wgu, wd, wdt, wgut, sum_gu, sum_d, act_f, kept_f, kept_b,
           act, dgu, out_f, out_b, got_f, got_b, got_pass, sent_f, sent_b, sent_pass, saved, loaded, brought, stored, credit, room):
    me = lax.axis_index("pp")
    after, before = lax.rem(me + 1, STAGES), lax.rem(me + LAST, STAGES)
    first, last = me == 0, me == LAST

    def tokens(ref, p, n):
        return ref.at[p // 4, pl.ds(pl.multiple_of(lax.rem(p, 4) * 128, 128), n), :]

    def rows(p, n):
        return pl.ds(pl.multiple_of(p * 128, 128), n)

    def ring(p, n):
        return rows(lax.rem(p, 2 * RING), n)

    def deep(p, n):
        return rows(lax.rem(p, 4 * DEPTH), n)

    def whole(ref, m):
        return ref.at[rows(lax.rem(m, RING) * 2, LARGE), :]

    fetch = []
    for j in range(BLOCKS):
        fetch.append(pltpu.make_async_copy(wg_in.at[0, :, pl.ds(128 * j, 128)], wgu.at[:, pl.ds(256 * j, 128)], brought.at[2 * j]))
        fetch.append(pltpu.make_async_copy(wu_in.at[0, :, pl.ds(128 * j, 128)], wgu.at[:, pl.ds(256 * j + 128, 128)], brought.at[2 * j + 1]))
    fetch.append(pltpu.make_async_copy(wd_in.at[0], wd, brought.at[2 * BLOCKS]))
    for copy in fetch:
        copy.start()

    def local_f(p, n):
        return pltpu.make_async_copy(tokens(x, p, n), hs.at[rows(p, n), :], got_f.at[p])

    def local_b(p, n):
        return pltpu.make_async_copy(tokens(dy, p, n), dys.at[deep(p, n), :], got_b.at[p])

    def chunks(m):
        n = SMALL if m < HEAD or m >= MICRO - TAIL else LARGE
        return [(4 * m + r // 128, n) for r in range(0, T, n)]

    @pl.when(first)
    def _():
        for m in range(MICRO):
            for chunk in chunks(m):
                local_f(*chunk).start()

    @pl.when(last)
    def _():
        for m in range(DEPTH):
            for chunk in chunks(m):
                local_b(*chunk).start()

    barrier = pltpu.get_barrier_semaphore()
    links = [{i - 1, i + 1} & set(range(STAGES)) for i in range(STAGES)]
    for i, j in ((0, 3), (0, 4), (7, 4), (7, 3)):
        links[i].add(j)
        links[j].add(i)
    for i in range(STAGES):

        @pl.when(me == i)
        def _(i=i):
            for j in sorted(links[i]):
                pl.semaphore_signal(barrier, inc=1, device_id={"pp": j}, device_id_type=MESH)

    pl.semaphore_wait(barrier, pick(me, [len(link) for link in links]))
    for copy in fetch:
        copy.wait()

    def send(source, target, sent, got, device):
        return pltpu.make_async_remote_copy(source, target, sent, got, device_id={"pp": device}, device_id_type=MESH)

    def send_f(p, n):
        return send(out_f.at[ring(p, n), :], hs.at[rows(p, n), :], sent_f.at[lax.rem(p, 2 * RING)], got_f.at[p], after)

    def send_b(p, n):
        return send(out_b.at[ring(p, n), :], dys.at[deep(p, n), :], sent_b.at[lax.rem(p, 2 * RING)], got_b.at[p], before)

    def over_f(p):
        return send(out_f.at[ring(p, LARGE), :], whole(out_b, p // 4), sent_f.at[lax.rem(p, 2 * RING)], got_pass.at[lax.rem(p // 4, RING)], 0)

    def over_b(p):
        return send(out_b.at[ring(p, LARGE), :], whole(out_f, p // 4), sent_b.at[lax.rem(p, 2 * RING)], got_pass.at[lax.rem(p // 4, RING)], LAST)

    def pass_f(m):
        p = 4 * m + 2
        return send(whole(out_b, m), hs.at[rows(p, LARGE), :], sent_pass.at[lax.rem(m, RING)], got_f.at[p], 4)

    def pass_b(m):
        p = 4 * m + 2
        return send(whole(out_f, m), dys.at[deep(p, LARGE), :], sent_pass.at[lax.rem(m, RING)], got_b.at[p], 3)

    def saves(k, p, n):
        buffer = lax.rem(k, 2)
        return (pltpu.make_async_copy(kept_f.at[buffer, pl.ds(0, n), :], kept_far.at[rows(p, n), :], saved.at[2 * buffer]),
                pltpu.make_async_copy(act_f.at[buffer, pl.ds(0, n), :], act_far.at[rows(p, n), :], saved.at[2 * buffer + 1]))

    def loads(k, p, n):
        buffer, slot, part = lax.rem(k, 2), lax.rem(p // 4, SLOTS), rows(lax.rem(p, 4), n)
        return (pltpu.make_async_copy(kept_far.at[rows(p, n), :], kept_b.at[buffer, pl.ds(0, n), :], loaded.at[2 * buffer]),
                pltpu.make_async_copy(act_far.at[rows(p, n), :], act.at[slot, part, :], loaded.at[2 * buffer + 1]))

    def each_size(condition, p, do):
        for n in (LARGE, SMALL):

            @pl.when(condition & (is_small(p) if n == SMALL else jnp.logical_not(is_small(p))))
            def _(n=n):
                do(n)

    def wait_saved(condition, k):
        p = piece(k)

        def do(n):
            for copy in saves(k, p, n):
                copy.wait()

        each_size(condition, p, do)

    def load(condition, k, have_saved):
        p = piece(k)
        with jax.named_scope("saved"):
            wait_saved(condition & (have_saved <= k), k)

        def do(n):
            for copy in loads(k, p, n):
                copy.start()

        each_size(condition, p, do)
        return jnp.where(condition, jnp.maximum(have_saved, k + 1), have_saved)

    def free_ring(copy, p, n):
        if n == LARGE:

            @pl.when((p >= 2 * RING) & (p < 2 * RING + 4 * HEAD))
            def _():
                copy(p - 2 * RING, SMALL).wait_send()
                copy(p - 2 * RING + 1, SMALL).wait_send()

            @pl.when(p >= 2 * RING + 4 * HEAD)
            def _():
                copy(p - 2 * RING, LARGE).wait_send()
        else:

            @pl.when((p >= TAIL_AT) & (lax.rem(p, 2) == 0))
            def _():
                copy(p - 2 * RING, LARGE).wait_send()

    def inside(m, over):
        return (m >= over.start) & (m < over.stop)

    def passed(condition, m):
        with jax.named_scope("passed"):

            @pl.when(condition)
            def _():
                pass_f(m).wait_send()

            @pl.when(condition & first & inside(m + RING, OVER_F))
            def _():
                pl.semaphore_signal(credit, inc=1, device_id={"pp": 3}, device_id_type=MESH)

            @pl.when(condition & last & inside(m + RING, OVER_B))
            def _():
                pl.semaphore_signal(credit, inc=1, device_id={"pp": 4}, device_id_type=MESH)

    def take_forward(k, p, n, have_saved):
        with jax.named_scope("f_wait"):
            local_f(p, n).wait()
        with jax.named_scope("f_free"):
            free_ring(send_f, p, n)
            wait_saved((k >= 2) & (have_saved <= k - 2), k - 2)
        with jax.named_scope("f"):
            buffer = lax.rem(k, 2)
            out_f[ring(p, n), :] = forward(hs[rows(p, n), :], wgu, wd, act_f.at[buffer, pl.ds(0, n), :], kept_f.at[buffer, pl.ds(0, n), :])
            via = jnp.bool_(False)
            if n == LARGE and len(OVER_F):
                m = p // 4
                via = (me == 3) & (lax.rem(p, 4) == 2) & inside(m, OVER_F)

                @pl.when(via & (m >= OVER_F.start + RING))
                def _():
                    pl.semaphore_wait(credit, 1)

                @pl.when(via)
                def _():
                    over_f(p).start()

            @pl.when(jnp.logical_not(via))
            def _():
                send_f(p, n).start()

            for copy in saves(k, p, n):
                copy.start()

    def take_backward(k, p, n):
        m, part = p // 4, rows(lax.rem(p, 4), n)
        slot, buffer = lax.rem(m, SLOTS), lax.rem(k, 2)
        act_c, dgu_c, kept = act.at[slot, part, :], dgu.at[slot, part, :], kept_b.at[buffer, pl.ds(0, n), :]
        with jax.named_scope("b"):
            h, by = hs.at[rows(p, n), :], dys.at[deep(p, n), :]

            @pl.when(first)
            def _():
                backward(h[...], by[...], wgu, wdt, wgut, act_c, dgu_c, kept, False)

            @pl.when(jnp.logical_not(first))
            def _():
                @pl.when((m >= DEPTH) & (lax.rem(p, 4) == 0))
                def _():
                    pl.semaphore_wait(room, 1)

                free_ring(send_b, p, n)

            @pl.when(last)
            def _():
                out_b[ring(p, n), :] = backward(h[...], by[...], wgu, wdt, wgut, act_c, dgu_c, None, True)

            @pl.when(jnp.logical_not(first | last))
            def _():
                out_b[ring(p, n), :] = backward(h[...], by[...], wgu, wdt, wgut, act_c, dgu_c, kept, True)

            via = jnp.bool_(False)
            if n == LARGE and len(OVER_B):
                via = (me == 4) & (lax.rem(p, 4) == 2) & inside(m, OVER_B)

                @pl.when(via & (m >= OVER_B.start + RING))
                def _():
                    pl.semaphore_wait(credit, 1)

                @pl.when(via)
                def _():
                    over_b(p).start()

            @pl.when(jnp.logical_not(first | via))
            def _():
                send_b(p, n).start()

    def take_weights(m):
        slot, part = lax.rem(m, SLOTS), pl.ds(pl.multiple_of(m * T, T), T)
        by_weights(hs[part, :], dys[deep(4 * m, T), :], act.at[slot], dgu.at[slot], sum_gu, sum_d)

        @pl.when((m < MICRO - DEPTH) & jnp.logical_not(last))
        def _():
            pl.semaphore_signal(room, inc=1, device_id={"pp": after}, device_id_type=MESH)

        for later in range(DEPTH, MICRO):

            @pl.when(last & (m == later - DEPTH))
            def _(later=later):
                for chunk in chunks(later):
                    local_b(*chunk).start()

    def prepare():
        with jax.named_scope("init"):
            for j in range(BLOCKS):
                wgut[256 * j : 256 * j + 256, :] = wgu[:, 256 * j : 256 * j + 256].T
            for start in range(0, FF, 256):
                at_s = slice(start, min(start + 256, FF))
                wdt[:, at_s] = wd[at_s, :].T
            sum_gu[...] = jnp.zeros_like(sum_gu)
            sum_d[...] = jnp.zeros_like(sum_d)

    def step(s, carry):
        digits, n_f, n_b, n_w, n_p, n_saved, n_loaded = carry
        digit, digits = lax.rem(digits, 16), digits // 16
        do_f, do_b, do_w, do_p = (lax.rem(digit // d, 2) for d in (1, 2, 4, 8))
        keeps = jnp.logical_not(last)

        @pl.when(s == jnp.where(first, INIT_AT, 0))
        def _():
            prepare()

        if len(OVER_F) or len(OVER_B):
            begin = jnp.where(first, OVER_F.start, OVER_B.start)

            @pl.when(do_p == 1)
            def _():
                m = begin + n_p
                passed(n_p > 0, m - 1)
                with jax.named_scope("pass"):
                    pltpu.make_async_copy(tokens(x, 4 * m, LARGE), whole(out_b, m), got_pass.at[lax.rem(m, RING)]).wait()

                    @pl.when(first)
                    def _():
                        pass_f(m).start()

                    @pl.when(last)
                    def _():
                        pass_b(m).start()

        p = piece(n_f)
        each_size(do_f == 1, p, lambda n: take_forward(n_f, p, n, n_saved))
        n_saved = jnp.where((do_f == 1) & (n_f >= 2), jnp.maximum(n_saved, n_f - 1), n_saved)
        n_f += do_f

        def can_load(known):
            return keeps & (n_loaded < known) & (n_loaded < n_b + 2) & (n_w > piece(n_loaded) // 4 - SLOTS)

        early = (do_f == 1) & can_load(n_f - 1)
        n_saved = load(early, n_loaded, n_saved)
        n_loaded += early.astype(jnp.int32)

        c = piece(n_b)

        def arrive(n):
            with jax.named_scope("b_wait"):
                local_b(c, n).wait()

                @pl.when(last)
                def _():
                    local_f(c, n).wait()

            with jax.named_scope("b_load"):

                @pl.when(keeps)
                def _():
                    for copy in loads(n_b, c, n):
                        copy.wait()

        late = (do_b == 1) & keeps & (n_loaded == n_b)
        n_saved = load(late, n_loaded, n_saved)
        n_loaded += late.astype(jnp.int32)
        each_size(do_b == 1, c, arrive)
        beside = (do_b == 1) & can_load(n_f - do_f)
        n_saved = load(beside, n_loaded, n_saved)
        n_loaded += beside.astype(jnp.int32)
        each_size(do_b == 1, c, lambda n: take_backward(n_b, c, n))
        n_b += do_b
        behind = (do_b == 1) & can_load(n_f)
        n_saved = load(behind, n_loaded, n_saved)
        n_loaded += behind.astype(jnp.int32)

        @pl.when(do_w == 1)
        def _():
            with jax.named_scope("w"):
                take_weights(n_w)

        return digits, n_f, n_b, n_w + do_w, n_p + do_p, n_saved, n_loaded

    def word(i, carry):
        line, state = carry
        state = lax.fori_loop(i * WORD, i * WORD + WORD, step, (line[0], *state))
        return (*line[1:], line[0]), state[1:]

    lengths = [len(steps(order)) for order in ORDER]
    count = -(-max(lengths) // WORD)
    line = tuple(pick(me, values) for values in zip(*(words(order, count) for order in ORDER), strict=True))
    zero = jnp.int32(0)
    state = lax.fori_loop(0, pick(me, [-(-n // WORD) for n in lengths]), word, (line, (zero,) * 6))[1]
    n_saved = state[4]

    for k in range(CHUNKS - 2, CHUNKS):
        wait_saved(jnp.logical_not(last) & (n_saved <= k), jnp.int32(k))
    for copy, here in ((send_f, last), (send_b, first)):

        @pl.when(jnp.logical_not(here))
        def _(copy=copy):
            for p in range(PIECES - 2 * RING, TAIL_AT, 2):
                copy(p, LARGE).wait_send()
            for p in range(TAIL_AT, PIECES):
                copy(p, SMALL).wait_send()

    if len(OVER_F):
        passed(first, jnp.int32(OVER_F.stop - 1))
    if len(OVER_B):
        passed(last, jnp.int32(OVER_B.stop - 1))

    stores = []
    for j in range(BLOCKS):
        cols = slice(256 * j, 256 * j + 256)
        dgu[0, :, cols] = sum_gu[:, cols].astype(BF16)
        stores.append(pltpu.make_async_copy(dgu.at[0, :, pl.ds(256 * j, 128)], dwg.at[0, :, pl.ds(128 * j, 128)], stored.at[2 * j]))
        stores.append(pltpu.make_async_copy(dgu.at[0, :, pl.ds(256 * j + 128, 128)], dwu.at[0, :, pl.ds(128 * j, 128)], stored.at[2 * j + 1]))
        stores[-2].start()
        stores[-1].start()
    wd[...] = sum_d[...].astype(BF16)
    stores.append(pltpu.make_async_copy(wd, dwd.at[0], stored.at[2 * BLOCKS]))
    stores[-1].start()
    for store in stores:
        store.wait()


def solution(mesh):
    def step(x, dy, w_gate, w_up, w_down):
        v, sem = pltpu.VMEM, pltpu.SemaphoreType.DMA
        return pl.pallas_call(
            kernel,
            out_shape=[jax.ShapeDtypeStruct(w.shape, w.dtype) for w in (w_gate, w_up, w_down)]
            + [jax.ShapeDtypeStruct((MICRO * T, 2 * FF), F32), jax.ShapeDtypeStruct((MICRO * T, FF), BF16)],
            in_specs=[pl.BlockSpec(memory_space=pl.ANY)] * 5,
            out_specs=[pl.BlockSpec(memory_space=pl.ANY)] * 5,
            scratch_shapes=[
                v((MICRO * T, D), BF16), v((DEPTH * T, D), BF16),
                v((D, 2 * FF), BF16), v((FF, D), BF16), v((D, FF), BF16), v((2 * FF, D), BF16),
                v((D, 2 * FF), F32), v((FF, D), F32),
                v((2, LARGE, FF), BF16), v((2, LARGE, 2 * FF), F32), v((2, LARGE, 2 * FF), F32),
                v((SLOTS, T, FF), BF16), v((SLOTS, T, 2 * FF), BF16),
                v((RING * LARGE, D), BF16), v((RING * LARGE, D), BF16),
                sem((PIECES,)), sem((PIECES,)), sem((RING,)), sem((2 * RING,)), sem((2 * RING,)), sem((RING,)),
                sem((4,)), sem((4,)), sem((2 * BLOCKS + 1,)), sem((2 * BLOCKS + 1,)), pltpu.SemaphoreType.REGULAR, pltpu.SemaphoreType.REGULAR,
            ],
            compiler_params=pltpu.CompilerParams(collective_id=0, has_side_effects=True, vmem_limit_bytes=67043328),
        )(x, dy, w_gate, w_up, w_down)[:3]

    return jax.shard_map(
        step,
        mesh=mesh,
        in_specs=(P("rep", None, None),) * 2 + (P("pp", None, None),) * 3,
        out_specs=(P(("rep", "pp"), None, None),) * 3,
        check_vma=False,
    )
```

time: 265 us -> 234 us (0.88)
  Pallas kernels: 258 us -> 227 us
    pallas_call x1, Pallas kernels: 258 us -> 227 us  [step(): pl.pallas_call(kernel, out_shape=[jax.ShapeDtypeStruct(w.shape, w.dtype)...]
where the time goes in v2:
time: 234 us
  Pallas kernels  227 us (97%)
  local copies, waits for them, and re-layouts  6.15 us (3%)
    pallas_call x1, Pallas kernels, step(): pl.pallas_call(kernel, out_shape=[jax.ShapeDtypeStruct(w.shape, w.dtype)...  227 us
    unnamed x7, local copies, waits for them, and re-layouts  6.15 us

profile of v2, /device:TPU:0, one launch (start us, length us, event | category | flops | bytes accessed | tf_op | source)
XLA Modules:
  0.0 233.5 jit_solution(14914742857416311135)
XLA Ops:
  0.6 226.8 %shard_map.76 = (bf16[1,512,1664]{2,1,0:T(8,128)(2,1)}, bf16[1,512,1664]{2,1,0:T(8,128)(2,1)}, bf16[1,1664,512]{2,1,0:T(8,128)(2,1)}, f32[8192,3328]{1,0:T(8,128)}, bf16[8192,1664]{1,0:T(8,128)(2,1)}) custom-call(bf16[16,512,512]{2,1,0:T(8,128)(2,1)} %x.1, bf16[16,512,512]{2,1,0:T(8,128)(2,1)} %dy.1, bf16[1,512,1664]{2,1,0:T(8,128)(2,1)} %wg_in.1, ...), custom_call_target="tpu_custom_call" | custom-call | tf_op jit(solution)/shard_map/pallas_call | solution.py:517
  227.4 0.0 copy-start.1
  227.4 2.9 %copy.11 = bf16[1,512,1664]{2,1,0:T(8,128)(2,1)} copy(bf16[1,512,1664]{2,1,0:T(8,128)(2,1)} %get-tuple-element.12) | data formatting | bytes 3407872
  230.3 0.0 copy-done.1
  230.3 0.0 copy-start
  230.3 1.2 copy.12
  231.5 0.9 copy-done
  232.4 1.2 copy.13
Async XLA Ops:
  227.4 2.9 %copy-start.1 = (bf16[1,512,1664]{2,1,0:T(8,128)(2,1)S(1)}, bf16[1,512,1664]{2,1,0:T(8,128)(2,1)}, u32[]{:S(2)}) copy-start(bf16[1,512,1664]{2,1,0:T(8,128)(2,1)} %get-tuple-element.13) | copy-start | bytes 5111812
  230.3 2.1 copy-start

commit v3 on v2

--- a/solution.py
+++ b/solution.py
@@ -15,16 +15,16 @@
 RING = 4
 SLOTS = 3
 DEPTH = 6
-OVER_F, OVER_B = range(1, 15), range(0)
+OVER_F, OVER_B = range(2, 15), range(1, 13)
 ORDER = (
-    (0x181911911111111111111, 0x12512A831191111A93A19, 0x1622624622C25A235A22C, 0x1626222626622624),
-    (0x113311111111111111111, 0x152251113263137112311, 0x162626262626626224522, 0x14622222),
-    (0x113311313111111111111, 0x125225326353252531253, 0x122222622262625226353, 0x1446),
-    (0x131513313311111111111, 0x152523235227347331253, 0x144622222626263266312),
-    (0x131271315331131311111, 0x125232522526316331635, 0x144622226272312737),
-    (0x131522713111533331111, 0x172735232631573266313, 0x144622273272312),
-    (0x133723512317137223111, 0x172352337527336371316, 0x144622317132),
-    (0x166222622622466222222, 0x16224622622266224662),
+    (0x198911111111111111111, 0x1A1239898191119119111, 0x12224622C2226246A1622, 0x1622262666226226246),
+    (0x111111111111111111111, 0x122553331523633331111, 0x122626262626262626266, 0x146222),
+    (0x112311111111111111111, 0x126512225751313223111, 0x122626262263625235226, 0x14462222),
+    (0x131733131111111111111, 0x123663136225331712711, 0x14622622622626362635),
+    (0x153353317331131111111, 0x132523632671233712712, 0x1622662725226251),
+    (0x153335325131223111111, 0x171272712312772723513, 0x1462227272522712),
+    (0x112535233152311623311, 0x172312527377327377333, 0x14463325233),
+    (0x16A26A24C226622226222, 0x14622AE2E2A24EA2A2EE2, 0x14),
 )
 WORD = 7
 INIT_AT = 8
@@ -119,23 +119,24 @@
 def by_weights(h, dy, act, dgu, sum_gu, sum_d):
     wide = h.astype(F32)
     at = (wide * scale_of(wide)).astype(BF16).T
+    for start in range(0, FF, 256):
+        rows = slice(start, min(start + 256, FF))
+        sum_d[rows, :] += dot_rows(act[:, rows], dy).astype(BF16).astype(F32)
     for j in range(BLOCKS):
         at_j = slice(256 * j, 256 * j + 256)
         sum_gu[:, at_j] += dot(at, dgu[:, at_j]).astype(BF16).astype(F32)
-    for start in range(0, FF, 256):
-        rows = slice(start, min(start + 256, FF))
-        sum_d[rows, :] += dot_rows(act[:, rows], dy).astype(BF16).astype(F32)
 
 
 def pick(me, values):
     return sum(jnp.where(me == i, v, 0) for i, v in enumerate(values))
 
 
-def kernel(x, dy, wg_in, wu_in, wd_in, dwg, dwu, dwd, kept_far, act_far, hs, dys, wgu, wd, wdt, wgut, sum_gu, sum_d, act_f, kept_f, kept_b,
-           act, dgu, out_f, out_b, got_f, got_b, got_pass, sent_f, sent_b, sent_pass, saved, loaded, brought, stored, credit, room):
+def kernel(x, dy, wg_in, wu_in, wd_in, dwg, dwu, dwd, kept_far, act_far, hs, dys, wgu, wgut, sum_gu, sum_d, kept_f, kept_b,
+           act, dgu, out_f, out_b, got_f, got_b, got_pass, sent_f, sent_b, sent_pass, saved, loaded, brought, credit, room):
     me = lax.axis_index("pp")
     after, before = lax.rem(me + 1, STAGES), lax.rem(me + LAST, STAGES)
     first, last = me == 0, me == LAST
+    wdt, wd, act_f = dwg.at[0], dwd.at[0], dwu.at[0]
 
     def tokens(ref, p, n):
         return ref.at[p // 4, pl.ds(pl.multiple_of(lax.rem(p, 4) * 128, 128), n), :]
@@ -224,7 +225,7 @@
     def saves(k, p, n):
         buffer = lax.rem(k, 2)
         return (pltpu.make_async_copy(kept_f.at[buffer, pl.ds(0, n), :], kept_far.at[rows(p, n), :], saved.at[2 * buffer]),
-                pltpu.make_async_copy(act_f.at[buffer, pl.ds(0, n), :], act_far.at[rows(p, n), :], saved.at[2 * buffer + 1]))
+                pltpu.make_async_copy(act_f.at[rows(2 * buffer, n), :], act_far.at[rows(p, n), :], saved.at[2 * buffer + 1]))
 
     def loads(k, p, n):
         buffer, slot, part = lax.rem(k, 2), lax.rem(p // 4, SLOTS), rows(lax.rem(p, 4), n)
@@ -245,18 +246,24 @@
             for copy in saves(k, p, n):
                 copy.wait()
 
-        each_size(condition, p, do)
+        @pl.when(condition)
+        def _():
+            each_size(True, p, do)
 
     def load(condition, k, have_saved):
         p = piece(k)
-        with jax.named_scope("saved"):
-            wait_saved(condition & (have_saved <= k), k)
-
-        def do(n):
-            for copy in loads(k, p, n):
-                copy.start()
-
-        each_size(condition, p, do)
+
+        @pl.when(condition)
+        def _():
+            with jax.named_scope("saved"):
+                wait_saved(have_saved <= k, k)
+
+            def do(n):
+                for copy in loads(k, p, n):
+                    copy.start()
+
+            each_size(True, p, do)
+
         return jnp.where(condition, jnp.maximum(have_saved, k + 1), have_saved)
 
     def free_ring(copy, p, n):
@@ -302,7 +309,7 @@
             wait_saved((k >= 2) & (have_saved <= k - 2), k - 2)
         with jax.named_scope("f"):
             buffer = lax.rem(k, 2)
-            out_f[ring(p, n), :] = forward(hs[rows(p, n), :], wgu, wd, act_f.at[buffer, pl.ds(0, n), :], kept_f.at[buffer, pl.ds(0, n), :])
+            out_f[ring(p, n), :] = forward(hs[rows(p, n), :], wgu, wd, act_f.at[rows(2 * buffer, n), :], kept_f.at[buffer, pl.ds(0, n), :])
             via = jnp.bool_(False)
             if n == LARGE and len(OVER_F):
                 m = p // 4
@@ -374,12 +381,14 @@
         def _():
             pl.semaphore_signal(room, inc=1, device_id={"pp": after}, device_id_type=MESH)
 
-        for later in range(DEPTH, MICRO):
-
-            @pl.when(last & (m == later - DEPTH))
-            def _(later=later):
-                for chunk in chunks(later):
-                    local_b(*chunk).start()
+        @pl.when(last & (m < MICRO - DEPTH))
+        def _():
+            for later in range(DEPTH, MICRO):
+
+                @pl.when(m == later - DEPTH)
+                def _(later=later):
+                    for chunk in chunks(later):
+                        local_b(*chunk).start()
 
     def prepare():
         with jax.named_scope("init"):
@@ -420,7 +429,11 @@
                         pass_b(m).start()
 
         p = piece(n_f)
-        each_size(do_f == 1, p, lambda n: take_forward(n_f, p, n, n_saved))
+
+        @pl.when(do_f == 1)
+        def _():
+            each_size(True, p, lambda n: take_forward(n_f, p, n, n_saved))
+
         n_saved = jnp.where((do_f == 1) & (n_f >= 2), jnp.maximum(n_saved, n_f - 1), n_saved)
         n_f += do_f
 
@@ -451,11 +464,15 @@
         late = (do_b == 1) & keeps & (n_loaded == n_b)
         n_saved = load(late, n_loaded, n_saved)
         n_loaded += late.astype(jnp.int32)
-        each_size(do_b == 1, c, arrive)
-        beside = (do_b == 1) & can_load(n_f - do_f)
-        n_saved = load(beside, n_loaded, n_saved)
-        n_loaded += beside.astype(jnp.int32)
-        each_size(do_b == 1, c, lambda n: take_backward(n_b, c, n))
+
+        @pl.when(do_b == 1)
+        def _():
+            def take(n):
+                arrive(n)
+                take_backward(n_b, c, n)
+
+            each_size(True, c, take)
+
         n_b += do_b
         behind = (do_b == 1) & can_load(n_f)
         n_saved = load(behind, n_loaded, n_saved)
@@ -496,19 +513,11 @@
     if len(OVER_B):
         passed(last, jnp.int32(OVER_B.stop - 1))
 
-    stores = []
     for j in range(BLOCKS):
-        cols = slice(256 * j, 256 * j + 256)
-        dgu[0, :, cols] = sum_gu[:, cols].astype(BF16)
-        stores.append(pltpu.make_async_copy(dgu.at[0, :, pl.ds(256 * j, 128)], dwg.at[0, :, pl.ds(128 * j, 128)], stored.at[2 * j]))
-        stores.append(pltpu.make_async_copy(dgu.at[0, :, pl.ds(256 * j + 128, 128)], dwu.at[0, :, pl.ds(128 * j, 128)], stored.at[2 * j + 1]))
-        stores[-2].start()
-        stores[-1].start()
-    wd[...] = sum_d[...].astype(BF16)
-    stores.append(pltpu.make_async_copy(wd, dwd.at[0], stored.at[2 * BLOCKS]))
-    stores[-1].start()
-    for store in stores:
-        store.wait()
+        block = slice(128 * j, 128 * j + 128)
+        dwg[0, :, block] = sum_gu[:, 256 * j : 256 * j + 128].astype(BF16)
+        dwu[0, :, block] = sum_gu[:, 256 * j + 128 : 256 * j + 256].astype(BF16)
+    dwd[0] = sum_d[...].astype(BF16)
 
 
 def solution(mesh):
@@ -516,21 +525,21 @@
         v, sem = pltpu.VMEM, pltpu.SemaphoreType.DMA
         return pl.pallas_call(
             kernel,
-            out_shape=[jax.ShapeDtypeStruct(w.shape, w.dtype) for w in (w_gate, w_up, w_down)]
+            out_shape=[pltpu.VMEM(w.shape, w.dtype) for w in (w_gate, w_up, w_down)]
             + [jax.ShapeDtypeStruct((MICRO * T, 2 * FF), F32), jax.ShapeDtypeStruct((MICRO * T, FF), BF16)],
             in_specs=[pl.BlockSpec(memory_space=pl.ANY)] * 5,
-            out_specs=[pl.BlockSpec(memory_space=pl.ANY)] * 5,
+            out_specs=[pl.BlockSpec(memory_space=pltpu.VMEM)] * 3 + [pl.BlockSpec(memory_space=pl.ANY)] * 2,
             scratch_shapes=[
                 v((MICRO * T, D), BF16), v((DEPTH * T, D), BF16),
-                v((D, 2 * FF), BF16), v((FF, D), BF16), v((D, FF), BF16), v((2 * FF, D), BF16),
+                v((D, 2 * FF), BF16), v((2 * FF, D), BF16),
                 v((D, 2 * FF), F32), v((FF, D), F32),
-                v((2, LARGE, FF), BF16), v((2, LARGE, 2 * FF), F32), v((2, LARGE, 2 * FF), F32),
+                v((2, LARGE, 2 * FF), F32), v((2, LARGE, 2 * FF), F32),
                 v((SLOTS, T, FF), BF16), v((SLOTS, T, 2 * FF), BF16),
                 v((RING * LARGE, D), BF16), v((RING * LARGE, D), BF16),
                 sem((PIECES,)), sem((PIECES,)), sem((RING,)), sem((2 * RING,)), sem((2 * RING,)), sem((RING,)),
-                sem((4,)), sem((4,)), sem((2 * BLOCKS + 1,)), sem((2 * BLOCKS + 1,)), pltpu.SemaphoreType.REGULAR, pltpu.SemaphoreType.REGULAR,
+                sem((4,)), sem((4,)), sem((2 * BLOCKS + 1,)), pltpu.SemaphoreType.REGULAR, pltpu.SemaphoreType.REGULAR,
             ],
-            compiler_params=pltpu.CompilerParams(collective_id=0, has_side_effects=True, vmem_limit_bytes=67043328),
+            compiler_params=pltpu.CompilerParams(collective_id=0, has_side_effects=True, vmem_limit_bytes=59 * 2**20 - 2**17),
         )(x, dy, w_gate, w_up, w_down)[:3]
 
     return jax.shard_map(

time: 234 us -> 228 us (0.974)
  Pallas kernels: 227 us -> 223 us
  local copies, waits for them, and re-layouts: 6.15 us -> 3.56 us
    pallas_call x1, Pallas kernels: 227 us -> 223 us  [step(): pl.pallas_call(kernel, out_shape=[pltpu.VMEM(w.shape, w.dtype) for w in (...]
    unnamed x7 -> x3, local copies, waits for them, and re-layouts: 6.15 us -> 3.56 us
where the time goes in v3:
time: 228 us
  Pallas kernels  223 us (98%)
  local copies, waits for them, and re-layouts  3.56 us (2%)
    pallas_call x1, Pallas kernels, step(): pl.pallas_call(kernel, out_shape=[pltpu.VMEM(w.shape, w.dtype) for w in (...  223 us

profile of v3, /device:TPU:0, one launch (start us, length us, event | category | flops | bytes accessed | tf_op | source)
XLA Modules:
  0.0 227.6 jit_solution(6609836451442300632)
XLA Ops:
  0.6 223.4 %shard_map.76 = (bf16[1,512,1664]{2,1,0:T(8,128)(2,1)S(1)}, bf16[1,512,1664]{2,1,0:T(8,128)(2,1)S(1)}, bf16[1,1664,512]{2,1,0:T(8,128)(2,1)S(1)}, f32[8192,3328]{1,0:T(8,128)}, bf16[8192,1664]{1,0:T(8,128)(2,1)}) custom-call(bf16[16,512,512]{2,1,0:T(8,128)(2,1)} %x.1, bf16[16,512,512]{2,1,0:T(8,128)(2,1)} %dy.1, bf16[1,512,1664]{2,1,0:T(8,128)(2,1)} %wg_in.1, ...), custom_call_target="tpu_custom_call" | custom-call | tf_op jit(solution)/shard_map/pallas_call | solution.py:526
  224.1 1.2 copy.11
  225.3 1.2 copy.12
  226.4 1.2 copy.13

commit v4 on v3

--- a/solution.py
+++ b/solution.py
@@ -15,16 +15,16 @@
 RING = 4
 SLOTS = 3
 DEPTH = 6
-OVER_F, OVER_B = range(2, 15), range(1, 13)
+OVER_F, OVER_B = range(1, 15), range(1, 10)
 ORDER = (
-    (0x198911111111111111111, 0x1A1239898191119119111, 0x12224622C2226246A1622, 0x1622262666226226246),
-    (0x111111111111111111111, 0x122553331523633331111, 0x122626262626262626266, 0x146222),
-    (0x112311111111111111111, 0x126512225751313223111, 0x122626262263625235226, 0x14462222),
-    (0x131733131111111111111, 0x123663136225331712711, 0x14622622622626362635),
-    (0x153353317331131111111, 0x132523632671233712712, 0x1622662725226251),
-    (0x153335325131223111111, 0x171272712312772723513, 0x1462227272522712),
-    (0x112535233152311623311, 0x172312527377327377333, 0x14463325233),
-    (0x16A26A24C226622226222, 0x14622AE2E2A24EA2A2EE2, 0x14),
+    (0x119199911111111111111, 0x12225113991B1A111B991, 0x12622666226266222C82C, 0x1626222666226),
+    (0x111111111111111111111, 0x144631332531123113311, 0x162626262626626622632, 0x14622222),
+    (0x131331111111111111111, 0x122663515233337251311, 0x122222626262262622653, 0x1446),
+    (0x162331111111111111111, 0x125252313631273153131, 0x122222626262622652327, 0x1446),
+    (0x171253331231111111111, 0x171733631325272713126, 0x14622262626363253),
+    (0x171631631731333111111, 0x125332573337373267313, 0x144622222736),
+    (0x165333737731313723131, 0x123271273123167377333, 0x14462335),
+    (0x1E62A62C6222462222222, 0x16222622C26AA22C62C2A, 0x146),
 )
 WORD = 7
 INIT_AT = 8

time: 228 us -> 227 us (level)
  no operation moved by 1% of the time
where the time goes in v4:
time: 227 us
  Pallas kernels  223 us (98%)
  local copies, waits for them, and re-layouts  3.56 us (2%)
    pallas_call x1, Pallas kernels, step(): pl.pallas_call(kernel, out_shape=[pltpu.VMEM(w.shape, w.dtype) for w in (...  223 us

profile of v4, /device:TPU:0, one launch (start us, length us, event | category | flops | bytes accessed | tf_op | source)
XLA Modules:
  0.0 226.8 jit_solution(13989272567003421735)
XLA Ops:
  0.6 222.6 %shard_map.76 = (bf16[1,512,1664]{2,1,0:T(8,128)(2,1)S(1)}, bf16[1,512,1664]{2,1,0:T(8,128)(2,1)S(1)}, bf16[1,1664,512]{2,1,0:T(8,128)(2,1)S(1)}, f32[8192,3328]{1,0:T(8,128)}, bf16[8192,1664]{1,0:T(8,128)(2,1)}) custom-call(bf16[16,512,512]{2,1,0:T(8,128)(2,1)} %x.1, bf16[16,512,512]{2,1,0:T(8,128)(2,1)} %dy.1, bf16[1,512,1664]{2,1,0:T(8,128)(2,1)} %wg_in.1, ...), custom_call_target="tpu_custom_call" | custom-call | tf_op jit(solution)/shard_map/pallas_call | solution.py:526
  223.3 1.2 copy.11
  224.4 1.2 copy.12
  225.6 1.2 copy.13
